TPU v7x, 256 devices: a whole 4x4x8 slice. The times are simulated.
256 devices in a mesh: loc: 32 (over y, x, core), tm: 8 (over z).
Axes of the slice: x: 4, y: 4, z: 8, core: 2. Of those that a mesh axis runs over, the one named last changes fastest.
Arguments:
- observed: float32 [4096, 1024], P('loc', 'tm'), may hold values from -6 to 6
- observed_mask: int32 [4096, 1024], P('loc', 'tm'), may hold values 0 or 1
- training_site_positions: float32 [2, 4096], replicated, may hold values from 0 to 1
- time_stamps: float32 [1024], replicated, may hold values from 0 to 1
- noise_var: float32 [1024], P('tm'), may hold values from 0.2 to 2
- test_coords: float32 [2, 4096], replicated, may hold values from 0 to 1
- site_order: int32 [4096], replicated, may hold values from 0 to 4095, each once
Outputs:
- solver_estimate: float32 [4096, 1024], P('loc', 'tm')
- posterior_mean_field: float32 [4096, 1024], P('loc', 'tm')
Inputs may be any that keep to these rules, and one draw needn't show every extreme that they name: `site_order`: each test site appears once.
All inputs are finite; a program needn't handle non-finite values. No bound on the sum of `observed_mask` on one device may be relied on, other than what follows from the above.
Results may differ from a plain program's by a relative error of at most 0.00022.
Values sent between devices are 32-bit elements; how exact they have to be, the bound alone decides.
No kernel may reach another device: no remote copies, remote signals or barrier semaphores. Data moves between devices by JAX's collectives and lax.ppermute only.
A program may use at most 64 MiB of HBM per device.

v0:
```python
import math
import jax
import jax.numpy as jnp
from jax import lax
from jax.sharding import Mesh
from jax.sharding import PartitionSpec as P

ITERS = 2
LOC = ("loc_0", "loc_1", "loc_2")
LOC_TM = ("loc_0", "loc_1", "loc_2", "tm")
root_three = math.sqrt(3.0)
space_reach = 2.5
time_reach = 5.0
covariance_times_iterate = 0.1


def from_everyone(shard, axis):
    copies = jnp.broadcast_to(shard, (lax.axis_size(axis), *shard.shape))
    return lax.all_to_all(copies, axis, split_axis=0, concat_axis=0, tiled=True)


def in_order(parts, dim):
    parts = jnp.moveaxis(parts, 0, dim)
    shape = parts.shape
    return parts.reshape(*shape[:dim], shape[dim] * shape[dim + 1], *shape[dim + 2 :])


def collect(shard, axis, dim):
    parts = from_everyone(shard, axis)
    return in_order(parts, dim)


def by_axis(shard, axes):
    for axis in axes:
        shard = lax.psum(shard, axis)
    return shard


def split_up(shard, dim, length):
    shape = shard.shape
    parts = shard.reshape(*shape[:dim], length, shape[dim] // length, *shape[dim + 1 :])
    return jnp.moveaxis(parts, dim, 0)


def summed_on_arrival(shard, axis, dim):
    parts = split_up(shard, dim, lax.axis_size(axis))
    arrived = lax.all_to_all(parts, axis, split_axis=0, concat_axis=0, tiled=True)
    return arrived.sum(axis=0)


def matern(left_points, right_points, length):
    squared = jnp.sum(jnp.square(left_points[:, :, None] - right_points[:, None, :]), axis=0)
    scaled = jnp.sqrt(squared) * (root_three / length)
    return (1.0 + scaled) * jnp.exp(-scaled)


def between_covariance_block(row_points, col_points, right_side, length):
    row_count = row_points.shape[1]
    block_size = math.gcd(row_count, 2048)
    number = row_count // block_size
    blocks = row_points.reshape(row_points.shape[0], number, block_size).transpose(1, 0, 2)

    def one_block(points):
        return jnp.dot(
            matern(points, col_points, length),
            right_side,
            precision=lax.Precision.HIGHEST,
            preferred_element_type=jnp.float32,
        )

    return lax.map(one_block, blocks).reshape(row_count, right_side.shape[1])


def column_sum(row_points, col_points, right_side, length):
    col_count = col_points.shape[1]
    block_size = math.gcd(col_count, 2048)
    number = col_count // block_size

    def add_block(index, summed):
        offset = index * block_size
        columns = lax.dynamic_slice_in_dim(col_points, offset, block_size, 1)
        rows_part = lax.dynamic_slice_in_dim(right_side, offset, block_size, 0)
        kernel = matern(row_points, columns, length)
        return summed + jnp.dot(
            kernel, rows_part, precision=lax.Precision.HIGHEST, preferred_element_type=jnp.float32
        )

    empty = jnp.zeros((row_points.shape[1], right_side.shape[1]), jnp.float32)
    return lax.fori_loop(0, number, add_block, empty)


def on_device(
    observed,
    observed_mask,
    training_site_positions,
    time_stamps,
    noise_var,
    test_coords,
    site_order,
):
    loc_rows = observed.shape[0]
    time_cols = observed.shape[1]
    mask_float = observed_mask.astype(jnp.float32)
    planar_correlation_range = space_reach / math.sqrt(training_site_positions.shape[1])
    time_length = time_reach / time_stamps.shape[0]
    own_points = lax.dynamic_slice_in_dim(
        training_site_positions, lax.axis_index(LOC) * loc_rows, loc_rows, 1
    )
    own_stamps = lax.dynamic_slice_in_dim(
        time_stamps, lax.axis_index("tm") * time_cols, time_cols, 0
    )

    def time_fold(shard_piece):
        kernel = matern(time_stamps[None, :], own_stamps[None, :], time_length)
        return jnp.dot(
            shard_piece, kernel, precision=lax.Precision.HIGHEST, preferred_element_type=jnp.float32
        )

    def squares(residual):
        return by_axis(jnp.sum(residual * residual), LOC_TM)

    solver_estimate = jnp.zeros_like(observed)
    residual = mask_float * observed
    direction = residual
    norm_now = squares(residual)
    for iteration in range(ITERS):
        masked = mask_float * direction
        inner = time_fold(collect(masked, "tm", 1))
        outer = column_sum(
            own_points, training_site_positions, collect(inner, LOC, 0), planar_correlation_range
        )
        image = mask_float * outer * covariance_times_iterate + direction * noise_var[None, :]
        curvature_sum = by_axis(jnp.sum(direction * image), LOC_TM)
        step_size = norm_now / curvature_sum
        solver_estimate = solver_estimate + step_size * direction
        residual = residual - step_size * image
        if iteration + 1 < ITERS:
            norm_next = squares(residual)
            direction = residual + norm_next / norm_now * direction
            norm_now = norm_next
    temporal_observation_grid = time_fold(collect(solver_estimate, "tm", 1))
    unseen_site_positions = test_coords[:, site_order]
    local_share = summed_on_arrival(
        between_covariance_block(
            unseen_site_positions, own_points, temporal_observation_grid, planar_correlation_range
        ),
        LOC,
        0,
    )
    posterior_mean_field = local_share * covariance_times_iterate
    return (solver_estimate, posterior_mean_field)


def solution(mesh):
    split = Mesh(mesh.devices.reshape(4, 4, 2, mesh.shape["tm"]), ("loc_0", "loc_1", "loc_2", "tm"))
    in_specs = (P(LOC, "tm"), P(LOC, "tm"), P(), P(), P("tm"), P(), P())
    out_specs = (P(LOC, "tm"), P(LOC, "tm"))
    return jax.shard_map(
        on_device, mesh=split, in_specs=in_specs, out_specs=out_specs, check_vma=False
    )
```

profile of v0, /device:TPU:1, one launch (start us, length us, event | category | flops | bytes accessed | tf_op | source)
XLA Modules:
  0.0 312.8 jit_solution(4415096766362854588)
XLA Ops:
  2.4 9.0 %all-to-all-start = ((f32[8,128,128]{1,2,0:T(8,128)}), f32[8,128,128]{1,2,0:T(8,128)S(1)}, u32[]{:S(2)}, u32[]{:S(2)}) async-start(f32[8,128,128]{1,2,0:T(8,128)} %broadcast_in_dim.41), calls=%async_computation | async-start | bytes 1048576 | tf_op jit(solution)/shard_map/all_to_all | solution.py:19
  12.2 17.2 %all-to-all-done = f32[8,128,128]{1,2,0:T(8,128)S(1)} async-done(((f32[8,128,128]{1,2,0:T(8,128)}), f32[8,128,128]{1,2,0:T(8,128)S(1)}, u32[]{:S(2)}, u32[]{:S(2)}) %all-to-all-start) | async-done | bytes 524320 | tf_op jit(solution)/shard_map/all_to_all | solution.py:19
  29.4 1.9 fusion.39
  31.3 1.6 broadcast_in_dim.42
  32.9 7.7 %all-to-all-start.1 = ((f32[32,128,128]{2,1,0:T(8,128)}), f32[32,128,128]{2,1,0:T(8,128)S(1)}, u32[]{:S(2)}, u32[]{:S(2)}) async-start(f32[32,128,128]{2,1,0:T(8,128)} %broadcast_in_dim.42), calls=%async_computation.1 | async-start | bytes 4194304 | tf_op jit(solution)/shard_map/all_to_all | solution.py:19
  40.7 28.5 %all-to-all-done.1 = f32[32,128,128]{2,1,0:T(8,128)S(1)} async-done(((f32[32,128,128]{2,1,0:T(8,128)}), f32[32,128,128]{2,1,0:T(8,128)S(1)}, u32[]{:S(2)}, u32[]{:S(2)}) %all-to-all-start.1) | async-done | bytes 2097184 | tf_op jit(solution)/shard_map/all_to_all | solution.py:19
  69.2 3.7 %while.39 = (s32[]{:T(128)}, f32[128,128]{1,0:T(8,128)S(1)}, f32[2,128]{1,0:T(2,128)S(1)}, f32[2,4096]{1,0:T(2,128)S(1)}, f32[4096,128]{1,0:T(8,128)S(1)}, /*index=5*/s32[]{:T(128)}, s32[]{:T(128)}, s32[]{:T(128)}, s32[]{:T(128)}) while((s32[]{:T(128)}, f32[128,128]{1,0:T(8,128)S(1)}, f32[2,128]{1,0:T(2,128)S(1)}, ...), condition=%wide.region_7.8_spmd.clone, body=%wide.region_5.7_spmd.clone.sunk | while | flops 405045248 | bytes 3327133 | solution.py:89
  71.4 1.6 convolution_add_fusion.4
  73.6 6.7 %all-reduce.2 = (f32[]{:T(128)}, f32[]{:T(128)}) all-reduce(f32[]{:T(128)} %get-tuple-element.257, f32[]{:T(128)} %get-tuple-element.256), channel_id=1, replica_groups=mesh['loc_0'=4,'loc_1'=4,'loc_2'=2,'tm'=8] {'loc_0'}, use_global_device_ids=true, to_apply=%region_1.0 | all-reduce | flops 2 | bytes 16 | tf_op jit(solution)/shard_map/psum | solution.py:35
  80.4 9.8 %all-reduce.1 = (f32[]{:T(128)}, f32[]{:T(128)}) all-reduce(f32[]{:T(128)} %get-tuple-element.292, f32[]{:T(128)} %get-tuple-element.293), channel_id=1, replica_groups=mesh['loc_0'=4,'loc_1'=4,'loc_2'=2,'tm'=8] {'loc_1'}, use_global_device_ids=true, to_apply=%region_2.0 | all-reduce | flops 2 | bytes 16 | tf_op jit(solution)/shard_map/psum | solution.py:35
  90.2 5.9 %all-reduce.3 = (f32[]{:T(128)}, f32[]{:T(128)}) all-reduce(f32[]{:T(128)} %get-tuple-element.290, f32[]{:T(128)} %get-tuple-element.291), channel_id=1, replica_groups=mesh['loc_0'=4,'loc_1'=4,'loc_2'=2,'tm'=8] {'loc_2'}, use_global_device_ids=true, to_apply=%region_3.0 | all-reduce | flops 2 | bytes 16 | tf_op jit(solution)/shard_map/psum | solution.py:35
  96.1 11.6 %all-reduce = (f32[]{:T(128)}, f32[]{:T(128)}) all-reduce(f32[]{:T(128)} %get-tuple-element.294, f32[]{:T(128)} %get-tuple-element.295), channel_id=1, replica_groups=mesh['loc_0'=4,'loc_1'=4,'loc_2'=2,'tm'=8] {'tm'}, use_global_device_ids=true, to_apply=%region_4.0 | all-reduce | flops 2 | bytes 16 | tf_op jit(solution)/shard_map/psum | solution.py:35
  109.6 7.2 %psum.120 = f32[]{:T(128)} all-reduce(f32[]{:T(128)} %multiply_reduce_fusion.4), channel_id=1, replica_groups=mesh['loc_0'=4,'loc_1'=4,'loc_2'=2,'tm'=8] {'loc_0'}, use_global_device_ids=true, to_apply=%region_14.0 | all-reduce | flops 1 | bytes 8 | tf_op jit(solution)/shard_map/psum | solution.py:35
  116.7 8.4 %psum.121 = f32[]{:T(128)} all-reduce(f32[]{:T(128)} %psum.120), channel_id=1, replica_groups=mesh['loc_0'=4,'loc_1'=4,'loc_2'=2,'tm'=8] {'loc_1'}, use_global_device_ids=true, to_apply=%region_15.0 | all-reduce | flops 1 | bytes 8 | tf_op jit(solution)/shard_map/psum | solution.py:35
  125.2 10.8 %psum.122 = f32[]{:T(128)} all-reduce(f32[]{:T(128)} %psum.121), channel_id=1, replica_groups=mesh['loc_0'=4,'loc_1'=4,'loc_2'=2,'tm'=8] {'loc_2'}, use_global_device_ids=true, to_apply=%region_16.0 | all-reduce | flops 1 | bytes 8 | tf_op jit(solution)/shard_map/psum | solution.py:35
  135.9 12.5 %psum.123 = f32[]{:T(128)} all-reduce(f32[]{:T(128)} %psum.122), channel_id=1, replica_groups=mesh['loc_0'=4,'loc_1'=4,'loc_2'=2,'tm'=8] {'tm'}, use_global_device_ids=true, to_apply=%region_17.0 | all-reduce | flops 1 | bytes 8 | tf_op jit(solution)/shard_map/psum | solution.py:35
  149.8 16.1 %all_to_all.30 = f32[8,128,128]{1,2,0:T(8,128)S(1)} all-to-all(f32[8,128,128]{1,2,0:T(8,128)S(1)} %broadcast_in_dim.43), channel_id=1, replica_groups=mesh['loc_0'=4,'loc_1'=4,'loc_2'=2,'tm'=8] {'tm'}, dimensions={0} | all-to-all | bytes 1048576 | tf_op jit(solution)/shard_map/all_to_all | solution.py:19
  167.2 1.6 broadcast_in_dim.44
  168.8 9.2 %all-to-all-start.3 = ((f32[32,128,128]{2,1,0:T(8,128)}), f32[32,128,128]{2,1,0:T(8,128)S(1)}, u32[]{:S(2)}, u32[]{:S(2)}) async-start(f32[32,128,128]{2,1,0:T(8,128)} %broadcast_in_dim.44), calls=%async_computation.3 | async-start | bytes 4194304 | tf_op jit(solution)/shard_map/all_to_all | solution.py:19
  177.9 28.3 %all-to-all-done.3 = f32[32,128,128]{2,1,0:T(8,128)S(1)} async-done(((f32[32,128,128]{2,1,0:T(8,128)}), f32[32,128,128]{2,1,0:T(8,128)S(1)}, u32[]{:S(2)}, u32[]{:S(2)}) %all-to-all-start.3) | async-done | bytes 2097184 | tf_op jit(solution)/shard_map/all_to_all | solution.py:19
  206.2 3.7 %while.40 = (s32[]{:T(128)}, f32[128,128]{1,0:T(8,128)S(1)}, f32[2,128]{1,0:T(2,128)S(1)}, f32[2,4096]{1,0:T(2,128)S(1)}, f32[4096,128]{1,0:T(8,128)S(1)}, /*index=5*/s32[]{:T(128)}, s32[]{:T(128)}, s32[]{:T(128)}, s32[]{:T(128)}) while((s32[]{:T(128)}, f32[128,128]{1,0:T(8,128)S(1)}, f32[2,128]{1,0:T(2,128)S(1)}, ...), condition=%wide.region_20.21_spmd.clone, body=%wide.region_18.20_spmd.clone.sunk | while | flops 405045248 | bytes 3327133 | solution.py:89
  210.7 7.0 %psum.124 = f32[]{:T(128)} all-reduce(f32[]{:T(128)} %multiply_reduce_fusion.3), channel_id=1, replica_groups=mesh['loc_0'=4,'loc_1'=4,'loc_2'=2,'tm'=8] {'loc_0'}, use_global_device_ids=true, to_apply=%region_22.0 | all-reduce | flops 1 | bytes 8 | tf_op jit(solution)/shard_map/psum | solution.py:35
  217.7 10.0 %psum.125 = f32[]{:T(128)} all-reduce(f32[]{:T(128)} %psum.124), channel_id=1, replica_groups=mesh['loc_0'=4,'loc_1'=4,'loc_2'=2,'tm'=8] {'loc_1'}, use_global_device_ids=true, to_apply=%region_23.0 | all-reduce | flops 1 | bytes 8 | tf_op jit(solution)/shard_map/psum | solution.py:35
  227.7 6.0 %psum.126 = f32[]{:T(128)} all-reduce(f32[]{:T(128)} %psum.125), channel_id=1, replica_groups=mesh['loc_0'=4,'loc_1'=4,'loc_2'=2,'tm'=8] {'loc_2'}, use_global_device_ids=true, to_apply=%region_24.0 | all-reduce | flops 1 | bytes 8 | tf_op jit(solution)/shard_map/psum | solution.py:35
  233.7 11.6 %psum.127 = f32[]{:T(128)} all-reduce(f32[]{:T(128)} %psum.126), channel_id=1, replica_groups=mesh['loc_0'=4,'loc_1'=4,'loc_2'=2,'tm'=8] {'tm'}, use_global_device_ids=true, to_apply=%region_25.0 | all-reduce | flops 1 | bytes 8 | tf_op jit(solution)/shard_map/psum | solution.py:35
  247.7 3.7 %all-to-all-start.4 = ((f32[8,128,128]{1,2,0:T(8,128)}), f32[8,128,128]{1,2,0:T(8,128)S(1)}, u32[]{:S(2)}, u32[]{:S(2)}) async-start(f32[8,128,128]{1,2,0:T(8,128)} %broadcast_in_dim.47), calls=%async_computation.4 | async-start | bytes 1048576 | tf_op jit(solution)/shard_map/all_to_all | solution.py:19
  252.1 14.1 %gather_fusion = f32[4096,2]{1,0:T(8,128)} fusion(f32[2,4096]{0,1:T(8,128)S(1)} %copy.23, s32[4096]{0:T(1024)S(1)} %fusion.53), kind=kCustom, calls=%fused_computation | custom fusion | bytes 81920 | tf_op jit(solution)/shard_map/gather | solution.py:142
  266.2 2.2 copy.24
  269.6 6.2 %while.38 = (s32[]{:T(128)}, f32[2,2048,128]{2,1,0:T(8,128)}, f32[2,2,2048]{2,1,0:T(2,128)S(1)}, f32[2,128]{1,0:T(2,128)S(1)}, f32[128,128]{1,0:T(8,128)S(1)}, /*index=5*/s32[]{:T(128)}) while((s32[]{:T(128)}, f32[2,2048,128]{2,1,0:T(8,128)}, f32[2,2,2048]{2,1,0:T(2,128)S(1)}, f32[2,128]{1,0:T(2,128)S(1)}, f32[128,128]{1,0:T(8,128)S(1)}, ...), condition=%wide.region_28.0_spmd, body=%wide.region_26.28_spmd.sunk | while | flops 405012480 | bytes 3262025 | solution.py:71
  270.4 2.3 fusion.73
  273.5 2.4 fusion.73
  275.9 36.2 %all_to_all.31 = f32[32,128,128]{2,1,0:T(8,128)S(1)} all-to-all(f32[32,128,128]{2,1,0:T(8,128)} %bitcast.42), channel_id=1, replica_groups=mesh['loc_0'=4,'loc_1'=4,'loc_2'=2,'tm'=8] {'loc_0','loc_1','loc_2'}, dimensions={0} | all-to-all | bytes 4194304 | tf_op jit(solution)/shard_map/all_to_all | solution.py:47
  (53 shorter events, 16.9 us)
Async XLA Ops:
  2.4 27.0 %all-to-all-start = ((f32[8,128,128]{1,2,0:T(8,128)}), f32[8,128,128]{1,2,0:T(8,128)S(1)}, u32[]{:S(2)}, u32[]{:S(2)}) async-start(f32[8,128,128]{1,2,0:T(8,128)} %broadcast_in_dim.41), calls=%async_computation | async-start | bytes 1048576 | tf_op jit(solution)/shard_map/all_to_all | solution.py:19
  32.9 7.7 %copy-start.1 = (f32[2,4096]{1,0:T(2,128)S(1)}, f32[2,4096]{1,0:T(2,128)}, u32[]{:S(2)}) copy-start(f32[2,4096]{1,0:T(2,128)} %param.15) | copy-start | bytes 98308
  32.9 36.3 %all-to-all-start.1 = ((f32[32,128,128]{2,1,0:T(8,128)}), f32[32,128,128]{2,1,0:T(8,128)S(1)}, u32[]{:S(2)}, u32[]{:S(2)}) async-start(f32[32,128,128]{2,1,0:T(8,128)} %broadcast_in_dim.42), calls=%async_computation.1 | async-start | bytes 4194304 | tf_op jit(solution)/shard_map/all_to_all | solution.py:19
  69.2 3.8 %copy-start = (s32[128,128]{1,0:T(8,128)S(1)}, s32[128,128]{1,0:T(8,128)}, u32[]{:S(2)}) copy-start(s32[128,128]{1,0:T(8,128)} %param.14) | copy-start | bytes 196612
  69.2 3.8 %copy-start.5 = (f32[128]{0:T(128)S(1)}, f32[128]{0:T(128)}, u32[]{:S(2)}) copy-start(f32[128]{0:T(128)} %param.17) | copy-start | bytes 1540
  73.0 92.9 %copy-start.6 = (f32[1024]{0:T(1024)S(1)}, f32[1024]{0:T(1024)}, u32[]{:S(2)}) copy-start(f32[1024]{0:T(1024)} %param.16) | copy-start | bytes 12292
  168.8 37.5 %all-to-all-start.3 = ((f32[32,128,128]{2,1,0:T(8,128)}), f32[32,128,128]{2,1,0:T(8,128)S(1)}, u32[]{:S(2)}, u32[]{:S(2)}) async-start(f32[32,128,128]{2,1,0:T(8,128)} %broadcast_in_dim.44), calls=%async_computation.3 | async-start | bytes 4194304 | tf_op jit(solution)/shard_map/all_to_all | solution.py:19
  210.0 41.4 %copy-start.3 = (f32[2,4096]{1,0:T(2,128)S(1)}, f32[2,4096]{1,0:T(2,128)}, u32[]{:S(2)}) copy-start(f32[2,4096]{1,0:T(2,128)} %param.18) | copy-start | bytes 98308
  210.7 41.3 %copy-start.4 = (s32[4096]{0:T(1024)S(1)}, s32[4096]{0:T(1024)}, u32[]{:S(2)}) copy-start(s32[4096]{0:T(1024)} %param.19) | copy-start | bytes 49156
  246.7 19.4 %copy-start.2 = (f32[128,128]{1,0:T(8,128)}, f32[128,128]{1,0:T(8,128)S(1)}, u32[]{:S(2)}) copy-start(f32[128,128]{1,0:T(8,128)S(1)} %multiply_add_fusion) | copy-start | bytes 196612
  247.7 20.7 %all-to-all-start.4 = ((f32[8,128,128]{1,2,0:T(8,128)}), f32[8,128,128]{1,2,0:T(8,128)S(1)}, u32[]{:S(2)}, u32[]{:S(2)}) async-start(f32[8,128,128]{1,2,0:T(8,128)} %broadcast_in_dim.47), calls=%async_computation.4 | async-start | bytes 1048576 | tf_op jit(solution)/shard_map/all_to_all | solution.py:19
where the time goes:
time: 314 us; the launch traced here: 313 us
  blocking collectives  160 us (51%)
  waiting for transfers between devices  74 us (24%)
  starting transfers between devices  29.6 us (9%)
  local copies, waits for them, and re-layouts  22.9 us (7%)
  matrix products  15.4 us (5%)
  other arithmetic  6.18 us (2%)
  between operations  4.74 us (2%)
    psum x12, blocking collectives, by_axis(): shard = lax.psum(shard, axis)  107 us
    all_to_all x4, waiting for transfers between devices, from_everyone(): return lax.all_to_all(copies, axis, split_axis=0, concat_axis=0, tiled=True)  74 us
    all_to_all x1, blocking collectives, summed_on_arrival(): lax.all_to_all(parts, axis, split_axis=0, concat_axis=0, tiled=True)  36.2 us
    all_to_all x4, starting transfers between devices, from_everyone(): return lax.all_to_all(copies, axis, split_axis=0, concat_axis=0, tiled=True)  29.6 us
    all_to_all x1, blocking collectives, from_everyone(): return lax.all_to_all(copies, axis, split_axis=0, concat_axis=0, tiled=True)  16.1 us
    gather x1, local copies, waits for them, and re-layouts, on_device(): unseen_site_positions = test_coords[:, site_order]  14.1 us
    dot_general x4, matrix products, add_block(): jnp.dot(kernel, rows_part, precision=lax.Precision.HIGHEST, preferred_ele...  6.34 us
  transfers between devices with their start and end apart: 4, of which 3 were waited for; matrix products, arithmetic and copies ran while one was open for 6% of the time, Pallas kernels for 0%

commit v1 on v0

--- a/solution.py
+++ b/solution.py
@@ -32,7 +32,8 @@
 
 def by_axis(shard, axes):
     for axis in axes:
-        shard = lax.psum(shard, axis)
+        pieces = lax.all_gather(shard, axis)
+        shard = jnp.sum(pieces, axis=0)
     return shard
 
 

time: 314 us -> 341 us (1.086)
  local copies, waits for them, and re-layouts: 22.9 us -> 47.4 us
  other arithmetic: 6.18 us -> 16.5 us
  blocking collectives: 160 us -> 152 us
    psum x12 -> x0, blocking collectives: 107 us -> none  [by_axis(): shard = lax.psum(shard, axis)]
    unnamed x0 -> x12, blocking collectives: none -> 99.4 us
    unnamed x15 -> x59, local copies, waits for them, and re-layouts: 0.68 us -> 25.2 us
    reduce_sum x0 -> x16, other arithmetic: none -> 10.2 us  [by_axis(): shard = jnp.sum(pieces, axis=0)]
  transfers between devices with their start and end apart: 4 -> 4, of which waited for: 3 -> 3; matrix products, arithmetic and copies ran while one was open for 6% -> 5% of each run, Pallas kernels for 0% -> 0%
where the time goes in v1:
time: 341 us; the launch traced here: 339 us
  blocking collectives  152 us (45%)
  waiting for transfers between devices  73.5 us (22%)
  local copies, waits for them, and re-layouts  47.4 us (14%)
  starting transfers between devices  29.6 us (9%)
  other arithmetic  16.5 us (5%)
  matrix products  15.5 us (5%)
  between operations  4.89 us (1%)
    unnamed x12, blocking collectives  99.4 us
    all_to_all x4, waiting for transfers between devices, from_everyone(): return lax.all_to_all(copies, axis, split_axis=0, concat_axis=0, tiled=True)  73.5 us
    all_to_all x1, blocking collectives, summed_on_arrival(): lax.all_to_all(parts, axis, split_axis=0, concat_axis=0, tiled=True)  36.2 us
    all_to_all x4, starting transfers between devices, from_everyone(): return lax.all_to_all(copies, axis, split_axis=0, concat_axis=0, tiled=True)  29.6 us
    unnamed x59, local copies, waits for them, and re-layouts  25.2 us
    all_to_all x1, blocking collectives, from_everyone(): return lax.all_to_all(copies, axis, split_axis=0, concat_axis=0, tiled=True)  16.1 us
    gather x1, local copies, waits for them, and re-layouts, on_device(): unseen_site_positions = test_coords[:, site_order]  14.1 us
    reduce_sum x16, other arithmetic, by_axis(): shard = jnp.sum(pieces, axis=0)  10.2 us
  transfers between devices with their start and end apart: 4, of which 3 were waited for; matrix products, arithmetic and copies ran while one was open for 5% of the time, Pallas kernels for 0%

profile of v1, /device:TPU:1, one launch (start us, length us, event | category | flops | bytes accessed | tf_op | source)
XLA Modules:
  0.0 339.2 jit_solution(5609335534036393890)
XLA Ops:
  2.4 9.0 %all-to-all-start = ((f32[8,128,128]{1,2,0:T(8,128)}), f32[8,128,128]{1,2,0:T(8,128)S(1)}, u32[]{:S(2)}, u32[]{:S(2)}) async-start(f32[8,128,128]{1,2,0:T(8,128)} %broadcast_in_dim.41), calls=%async_computation | async-start | bytes 1048576 | tf_op jit(solution)/shard_map/all_to_all | solution.py:19
  12.2 17.2 %all-to-all-done = f32[8,128,128]{1,2,0:T(8,128)S(1)} async-done(((f32[8,128,128]{1,2,0:T(8,128)}), f32[8,128,128]{1,2,0:T(8,128)S(1)}, u32[]{:S(2)}, u32[]{:S(2)}) %all-to-all-start) | async-done | bytes 524320 | tf_op jit(solution)/shard_map/all_to_all | solution.py:19
  29.4 1.9 fusion.39
  31.3 1.6 broadcast_in_dim.42
  32.9 7.7 %all-to-all-start.1 = ((f32[32,128,128]{2,1,0:T(8,128)}), f32[32,128,128]{2,1,0:T(8,128)S(1)}, u32[]{:S(2)}, u32[]{:S(2)}) async-start(f32[32,128,128]{2,1,0:T(8,128)} %broadcast_in_dim.42), calls=%async_computation.1 | async-start | bytes 4194304 | tf_op jit(solution)/shard_map/all_to_all | solution.py:19
  41.3 28.0 %all-to-all-done.1 = f32[32,128,128]{2,1,0:T(8,128)S(1)} async-done(((f32[32,128,128]{2,1,0:T(8,128)}), f32[32,128,128]{2,1,0:T(8,128)S(1)}, u32[]{:S(2)}, u32[]{:S(2)}) %all-to-all-start.1) | async-done | bytes 2097184 | tf_op jit(solution)/shard_map/all_to_all | solution.py:19
  69.3 3.8 %while.39 = (s32[]{:T(128)}, f32[128,128]{1,0:T(8,128)S(1)}, f32[2,128]{1,0:T(2,128)S(1)}, f32[2,4096]{1,0:T(2,128)S(1)}, f32[4096,128]{1,0:T(8,128)S(1)}, /*index=5*/s32[]{:T(128)}, s32[]{:T(128)}, s32[]{:T(128)}, s32[]{:T(128)}) while((s32[]{:T(128)}, f32[128,128]{1,0:T(8,128)S(1)}, f32[2,128]{1,0:T(2,128)S(1)}, ...), condition=%wide.region_7.8_spmd.clone, body=%wide.region_5.7_spmd.clone.sunk | while | flops 405045248 | bytes 3327133 | solution.py:90
  71.4 1.6 convolution_add_fusion.4
  77.2 6.0 %all-reduce.18 = (f32[4]{0:T(128)S(1)}, f32[4]{0:T(128)S(1)}) all-reduce(f32[4]{0:T(128)S(1)} %dynamic-update-slice, f32[4]{0:T(128)S(1)} %dynamic-update-slice.4), channel_id=1, replica_groups=mesh['loc_0'=4,'loc_1'=4,'loc_2'=2,'tm'=8] {'loc_0'}, use_global_device_ids=true, to_apply=%add | all-reduce | flops 8 | bytes 64
  87.8 9.2 %all-reduce.17 = (f32[4]{0:T(128)S(1)}, f32[4]{0:T(128)S(1)}) all-reduce(f32[4]{0:T(128)S(1)} %dynamic-update-slice.1, f32[4]{0:T(128)S(1)} %dynamic-update-slice.5), channel_id=1, replica_groups=mesh['loc_0'=4,'loc_1'=4,'loc_2'=2,'tm'=8] {'loc_1'}, use_global_device_ids=true, to_apply=%add.1 | all-reduce | flops 8 | bytes 64
  101.6 5.2 %all-reduce.19 = (f32[2]{0:T(128)S(1)}, f32[2]{0:T(128)S(1)}) all-reduce(f32[2]{0:T(128)S(1)} %dynamic-update-slice.2, f32[2]{0:T(128)S(1)} %dynamic-update-slice.6), channel_id=1, replica_groups=mesh['loc_0'=4,'loc_1'=4,'loc_2'=2,'tm'=8] {'loc_2'}, use_global_device_ids=true, to_apply=%add.2 | all-reduce | flops 4 | bytes 32
  110.8 10.9 %all-reduce.16 = (f32[8]{0:T(128)S(1)}, f32[8]{0:T(128)S(1)}) all-reduce(f32[8]{0:T(128)S(1)} %dynamic-update-slice.3, f32[8]{0:T(128)S(1)} %dynamic-update-slice.7), channel_id=1, replica_groups=mesh['loc_0'=4,'loc_1'=4,'loc_2'=2,'tm'=8] {'tm'}, use_global_device_ids=true, to_apply=%add.3 | all-reduce | flops 16 | bytes 128
  126.5 6.5 %all-reduce.8 = f32[4]{0:T(128)S(1)} all-reduce(f32[4]{0:T(128)S(1)} %dynamic-update-slice.8), channel_id=1, replica_groups=mesh['loc_0'=4,'loc_1'=4,'loc_2'=2,'tm'=8] {'loc_0'}, use_global_device_ids=true, to_apply=%add.8 | all-reduce | flops 4 | bytes 32
  135.1 7.7 %all-reduce.9 = f32[4]{0:T(128)S(1)} all-reduce(f32[4]{0:T(128)S(1)} %dynamic-update-slice.9), channel_id=1, replica_groups=mesh['loc_0'=4,'loc_1'=4,'loc_2'=2,'tm'=8] {'loc_1'}, use_global_device_ids=true, to_apply=%add.9 | all-reduce | flops 4 | bytes 32
  144.9 10.2 %all-reduce.10 = f32[2]{0:T(128)S(1)} all-reduce(f32[2]{0:T(128)S(1)} %dynamic-update-slice.10), channel_id=1, replica_groups=mesh['loc_0'=4,'loc_1'=4,'loc_2'=2,'tm'=8] {'loc_2'}, use_global_device_ids=true, to_apply=%add.10 | all-reduce | flops 2 | bytes 16
  157.2 11.8 %all-reduce.11 = f32[8]{0:T(128)S(1)} all-reduce(f32[8]{0:T(128)S(1)} %dynamic-update-slice.11), channel_id=1, replica_groups=mesh['loc_0'=4,'loc_1'=4,'loc_2'=2,'tm'=8] {'tm'}, use_global_device_ids=true, to_apply=%add.11 | all-reduce | flops 8 | bytes 64
  171.2 16.1 %all_to_all.30 = f32[8,128,128]{1,2,0:T(8,128)S(1)} all-to-all(f32[8,128,128]{1,2,0:T(8,128)S(1)} %broadcast_in_dim.43), channel_id=1, replica_groups=mesh['loc_0'=4,'loc_1'=4,'loc_2'=2,'tm'=8] {'tm'}, dimensions={0} | all-to-all | bytes 1048576 | tf_op jit(solution)/shard_map/all_to_all | solution.py:19
  188.5 1.6 broadcast_in_dim.44
  190.1 9.2 %all-to-all-start.3 = ((f32[32,128,128]{2,1,0:T(8,128)}), f32[32,128,128]{2,1,0:T(8,128)S(1)}, u32[]{:S(2)}, u32[]{:S(2)}) async-start(f32[32,128,128]{2,1,0:T(8,128)} %broadcast_in_dim.44), calls=%async_computation.3 | async-start | bytes 4194304 | tf_op jit(solution)/shard_map/all_to_all | solution.py:19
  199.3 28.3 %all-to-all-done.3 = f32[32,128,128]{2,1,0:T(8,128)S(1)} async-done(((f32[32,128,128]{2,1,0:T(8,128)}), f32[32,128,128]{2,1,0:T(8,128)S(1)}, u32[]{:S(2)}, u32[]{:S(2)}) %all-to-all-start.3) | async-done | bytes 2097184 | tf_op jit(solution)/shard_map/all_to_all | solution.py:19
  227.6 3.7 %while.40 = (s32[]{:T(128)}, f32[128,128]{1,0:T(8,128)S(1)}, f32[2,128]{1,0:T(2,128)S(1)}, f32[2,4096]{1,0:T(2,128)S(1)}, f32[4096,128]{1,0:T(8,128)S(1)}, /*index=5*/s32[]{:T(128)}, s32[]{:T(128)}, s32[]{:T(128)}, s32[]{:T(128)}) while((s32[]{:T(128)}, f32[128,128]{1,0:T(8,128)S(1)}, f32[2,128]{1,0:T(2,128)S(1)}, ...), condition=%wide.region_20.21_spmd.clone, body=%wide.region_18.20_spmd.clone.sunk | while | flops 405045248 | bytes 3327133 | solution.py:90
  233.4 6.3 %all-reduce.12 = f32[4]{0:T(128)S(1)} all-reduce(f32[4]{0:T(128)S(1)} %dynamic-update-slice.12), channel_id=1, replica_groups=mesh['loc_0'=4,'loc_1'=4,'loc_2'=2,'tm'=8] {'loc_0'}, use_global_device_ids=true, to_apply=%add.12 | all-reduce | flops 4 | bytes 32
  241.8 9.3 %all-reduce.13 = f32[4]{0:T(128)S(1)} all-reduce(f32[4]{0:T(128)S(1)} %dynamic-update-slice.13), channel_id=1, replica_groups=mesh['loc_0'=4,'loc_1'=4,'loc_2'=2,'tm'=8] {'loc_1'}, use_global_device_ids=true, to_apply=%add.13 | all-reduce | flops 4 | bytes 32
  253.1 5.2 %all-reduce.14 = f32[2]{0:T(128)S(1)} all-reduce(f32[2]{0:T(128)S(1)} %dynamic-update-slice.14), channel_id=1, replica_groups=mesh['loc_0'=4,'loc_1'=4,'loc_2'=2,'tm'=8] {'loc_2'}, use_global_device_ids=true, to_apply=%add.14 | all-reduce | flops 2 | bytes 16
  260.2 10.9 %all-reduce.15 = f32[8]{0:T(128)S(1)} all-reduce(f32[8]{0:T(128)S(1)} %dynamic-update-slice.15), channel_id=1, replica_groups=mesh['loc_0'=4,'loc_1'=4,'loc_2'=2,'tm'=8] {'tm'}, use_global_device_ids=true, to_apply=%add.15 | all-reduce | flops 8 | bytes 64
  274.1 3.7 %all-to-all-start.4 = ((f32[8,128,128]{1,2,0:T(8,128)}), f32[8,128,128]{1,2,0:T(8,128)S(1)}, u32[]{:S(2)}, u32[]{:S(2)}) async-start(f32[8,128,128]{1,2,0:T(8,128)} %broadcast_in_dim.47), calls=%async_computation.4 | async-start | bytes 1048576 | tf_op jit(solution)/shard_map/all_to_all | solution.py:19
  278.5 14.1 %gather_fusion = f32[4096,2]{1,0:T(8,128)} fusion(f32[2,4096]{0,1:T(8,128)S(1)} %copy.23, s32[4096]{0:T(1024)S(1)} %fusion.53), kind=kCustom, calls=%fused_computation | custom fusion | bytes 81920 | tf_op jit(solution)/shard_map/gather | solution.py:143
  292.5 2.2 copy.24
  296.0 6.2 %while.38 = (s32[]{:T(128)}, f32[2,2048,128]{2,1,0:T(8,128)}, f32[2,2,2048]{2,1,0:T(2,128)S(1)}, f32[2,128]{1,0:T(2,128)S(1)}, f32[128,128]{1,0:T(8,128)S(1)}, /*index=5*/s32[]{:T(128)}) while((s32[]{:T(128)}, f32[2,2048,128]{2,1,0:T(8,128)}, f32[2,2,2048]{2,1,0:T(2,128)S(1)}, f32[2,128]{1,0:T(2,128)S(1)}, f32[128,128]{1,0:T(8,128)S(1)}, ...), condition=%wide.region_28.0_spmd, body=%wide.region_26.28_spmd.sunk | while | flops 405012480 | bytes 3262025 | solution.py:72
  296.8 2.3 fusion.73
  299.9 2.3 fusion.73
  302.3 36.2 %all_to_all.31 = f32[32,128,128]{2,1,0:T(8,128)S(1)} all-to-all(f32[32,128,128]{2,1,0:T(8,128)} %bitcast.62), channel_id=1, replica_groups=mesh['loc_0'=4,'loc_1'=4,'loc_2'=2,'tm'=8] {'loc_0','loc_1','loc_2'}, dimensions={0} | all-to-all | bytes 4194304 | tf_op jit(solution)/shard_map/all_to_all | solution.py:48
  (113 shorter events, 51.8 us)
Async XLA Ops:
  2.4 27.0 %all-to-all-start = ((f32[8,128,128]{1,2,0:T(8,128)}), f32[8,128,128]{1,2,0:T(8,128)S(1)}, u32[]{:S(2)}, u32[]{:S(2)}) async-start(f32[8,128,128]{1,2,0:T(8,128)} %broadcast_in_dim.41), calls=%async_computation | async-start | bytes 1048576 | tf_op jit(solution)/shard_map/all_to_all | solution.py:19
  32.9 7.7 %copy-start.10 = (u32[256]{0:T(256)S(1)}, u32[256]{0:T(256)}, u32[]{:S(2)}) copy-start(u32[256]{0:T(256)} %constant.151) | copy-start | bytes 3076
  32.9 8.3 %copy-start.1 = (f32[2,4096]{1,0:T(2,128)S(1)}, f32[2,4096]{1,0:T(2,128)}, u32[]{:S(2)}) copy-start(f32[2,4096]{1,0:T(2,128)} %param.15) | copy-start | bytes 98308
  32.9 36.3 %all-to-all-start.1 = ((f32[32,128,128]{2,1,0:T(8,128)}), f32[32,128,128]{2,1,0:T(8,128)S(1)}, u32[]{:S(2)}, u32[]{:S(2)}) async-start(f32[32,128,128]{2,1,0:T(8,128)} %broadcast_in_dim.42), calls=%async_computation.1 | async-start | bytes 4194304 | tf_op jit(solution)/shard_map/all_to_all | solution.py:19
  69.2 3.8 %copy-start = (s32[128,128]{1,0:T(8,128)S(1)}, s32[128,128]{1,0:T(8,128)}, u32[]{:S(2)}) copy-start(s32[128,128]{1,0:T(8,128)} %param.14) | copy-start | bytes 196612
  69.2 3.8 %copy-start.5 = (f32[128]{0:T(128)S(1)}, f32[128]{0:T(128)}, u32[]{:S(2)}) copy-start(f32[128]{0:T(128)} %param.17) | copy-start | bytes 1540
  69.2 7.3 %copy-start.9 = (u32[256]{0:T(256)S(1)}, u32[256]{0:T(256)}, u32[]{:S(2)}) copy-start(u32[256]{0:T(256)} %constant.156) | copy-start | bytes 3076
  69.2 18.0 %copy-start.8 = (u32[256]{0:T(256)S(1)}, u32[256]{0:T(256)}, u32[]{:S(2)}) copy-start(u32[256]{0:T(256)} %constant.161) | copy-start | bytes 3076
  69.2 31.8 %copy-start.7 = (u32[256]{0:T(256)S(1)}, u32[256]{0:T(256)}, u32[]{:S(2)}) copy-start(u32[256]{0:T(256)} %constant.166) | copy-start | bytes 3076
  73.0 114.2 %copy-start.6 = (f32[1024]{0:T(1024)S(1)}, f32[1024]{0:T(1024)}, u32[]{:S(2)}) copy-start(f32[1024]{0:T(1024)} %param.16) | copy-start | bytes 12292
  190.1 37.5 %all-to-all-start.3 = ((f32[32,128,128]{2,1,0:T(8,128)}), f32[32,128,128]{2,1,0:T(8,128)S(1)}, u32[]{:S(2)}, u32[]{:S(2)}) async-start(f32[32,128,128]{2,1,0:T(8,128)} %broadcast_in_dim.44), calls=%async_computation.3 | async-start | bytes 4194304 | tf_op jit(solution)/shard_map/all_to_all | solution.py:19
  231.4 46.4 %copy-start.3 = (f32[2,4096]{1,0:T(2,128)S(1)}, f32[2,4096]{1,0:T(2,128)}, u32[]{:S(2)}) copy-start(f32[2,4096]{1,0:T(2,128)} %param.18) | copy-start | bytes 98308
  240.3 38.1 %copy-start.4 = (s32[4096]{0:T(1024)S(1)}, s32[4096]{0:T(1024)}, u32[]{:S(2)}) copy-start(s32[4096]{0:T(1024)} %param.19) | copy-start | bytes 49156
  273.1 19.4 %copy-start.2 = (f32[128,128]{1,0:T(8,128)}, f32[128,128]{1,0:T(8,128)S(1)}, u32[]{:S(2)}) copy-start(f32[128,128]{1,0:T(8,128)S(1)} %multiply_add_fusion) | copy-start | bytes 196612
  274.1 20.7 %all-to-all-start.4 = ((f32[8,128,128]{1,2,0:T(8,128)}), f32[8,128,128]{1,2,0:T(8,128)S(1)}, u32[]{:S(2)}, u32[]{:S(2)}) async-start(f32[8,128,128]{1,2,0:T(8,128)} %broadcast_in_dim.47), calls=%async_computation.4 | async-start | bytes 1048576 | tf_op jit(solution)/shard_map/all_to_all | solution.py:19
